TPU v7x, 32 devices: a whole 2x2x4 slice. The times are simulated.
32 devices in a mesh: slab: 8 (over z, x), rhs: 4 (over y, core).
Axes of the slice: x: 2, y: 2, z: 4, core: 2. Of those that a mesh axis runs over, the one named last changes fastest.
Arguments:
- targets: float32 [8, 128, 256], P('rhs', 'slab'), may hold values from -60 to 60
- counts: int32 [128], P('slab'), may hold values from 1 to 256, 20480 in all
- cell_rows: int32 [128, 256], P('slab'), may hold values from 0 to 255
- cell_cols: int32 [128, 256], P('slab'), may hold values from 0 to 127
- fractions: float32 [2, 128, 256], P(None, 'slab'), may hold values from 0 to 1
- spectrum: float32 [2048, 2048], P(None, ('slab', 'rhs')), may hold values from 0.25 to 4, as said below
- noise_var: float32 [1], replicated, may hold values from 0.1 to 1
Outputs:
- solution: float32 [8, 128, 256], P('rhs', 'slab')
- residual: float32 [8, 128, 256], P('rhs', 'slab')
Inputs may be any that keep to these rules, and one draw needn't show every extreme that they name: Each tile has 256 slots; tile t holds points in its first counts[t] slots, and the other slots are empty: their entries are ignored and their outputs are zero. Even in frequency: spectrum[a, b] = spectrum[(2048 - a) % 2048, (2048 - b) % 2048].
All inputs are finite; a program needn't handle non-finite values. No bound on the sum of `counts` on one device may be relied on, other than what follows from the above.
Results may differ from a plain program's by a relative error of at most 0.0002.
Values sent between devices are 32-bit elements; how exact they have to be, the bound alone decides.
No kernel may reach another device: no remote copies, remote signals or barrier semaphores. Data moves between devices by JAX's collectives and lax.ppermute only.
A program may use at most 128 MiB of HBM per device.

v0:
```python
import math

import jax
import jax.numpy as jnp
import ml_dtypes
import numpy as np
from jax import lax
from jax.experimental import pallas as pl
from jax.experimental.pallas import tpu as pltpu
from jax.sharding import PartitionSpec as P

G = 2048
TC = 128
ITERS = 2
WIN = 2 * TC
GEOM_ROWS = 24
VMEM_BYTES = 30 * 1024 * 1024


def cubic_weights(fraction):
    return (
        ((-0.5 * fraction + 1.0) * fraction - 0.5) * fraction,
        (1.5 * fraction - 2.5) * fraction * fraction + 1.0,
        ((-1.5 * fraction + 2.0) * fraction + 0.5) * fraction,
        (0.5 * fraction - 0.5) * fraction * fraction,
    )


def halves_np(table):
    high = table.astype(np.float32).astype(ml_dtypes.bfloat16)
    low = (table - high.astype(np.float64)).astype(np.float32).astype(ml_dtypes.bfloat16)
    return high, low


def angle_tables(rows, cols, length):
    index = (np.arange(rows)[:, None] * np.arange(cols)[None, :]) % length
    angle = index * (2.0 * math.pi / length)
    return np.cos(angle), np.sin(angle)


def row_matrices(size):
    cos_t, sin_t = angle_tables(size, size, size)
    out = []
    for sign in (1.0, -1.0):
        high, low = halves_np(np.block([[cos_t, sign * sin_t], [-sign * sin_t, cos_t]]))
        out.append(np.concatenate([high, high, low], axis=1))
    return out


def col_matrices(size):
    cos_t, sin_t = angle_tables(size, size, size)
    out = []
    for sign in (1.0, -1.0):
        high, low = halves_np(np.block([[cos_t, -sign * sin_t], [sign * sin_t, cos_t]]))
        out.append(np.concatenate([high, high, low], axis=0))
    return out


def halves(value):
    high = value.astype(jnp.bfloat16)
    low = (value - high.astype(jnp.float32)).astype(jnp.bfloat16)
    return high, low


def fft_list(real, imag, sign):
    count = len(real)
    if count == 1:
        return real, imag
    even_r, even_i = fft_list(real[0::2], imag[0::2], sign)
    odd_r, odd_i = fft_list(real[1::2], imag[1::2], sign)
    half = count // 2
    out_r, out_i = [None] * count, [None] * count
    for k in range(half):
        cos_k = math.cos(2.0 * math.pi * k / count)
        sin_k = sign * math.sin(2.0 * math.pi * k / count)
        if k == 0:
            turn_r, turn_i = odd_r[k], odd_i[k]
        elif 4 * k == count:
            turn_r, turn_i = -sign * odd_i[k], sign * odd_r[k]
        else:
            turn_r = odd_r[k] * cos_k - odd_i[k] * sin_k
            turn_i = odd_r[k] * sin_k + odd_i[k] * cos_k
        out_r[k], out_i[k] = even_r[k] + turn_r, even_i[k] + turn_i
        out_r[k + half], out_i[k + half] = even_r[k] - turn_r, even_i[k] - turn_i
    return out_r, out_i


def dot_f32(left, right, dims):
    return lax.dot_general(left, right, (dims, ((), ())), preferred_element_type=jnp.float32)


def wide(row):
    return jnp.broadcast_to(row, (16, row.shape[1])).astype(jnp.bfloat16)


def pick(hits, values):
    out = jnp.zeros(values[0].shape, values[0].dtype)
    for hit, value in zip(hits, values):
        out = jnp.where(hit, value, out)
    return out


def patterns(inner, value_rows):
    position = lax.broadcasted_iota(jnp.int32, (16, inner.shape[1]), 0).astype(jnp.float32)
    here = [position.astype(jnp.bfloat16) == wide(inner + float(tap)) for tap in range(4)]
    there = [position.astype(jnp.bfloat16) == wide(inner + float(tap - 16)) for tap in range(4)]
    return [(pick(here, values), pick(there, values)) for values in value_rows]


def split_rows(part):
    high = part.astype(jnp.bfloat16).astype(jnp.float32)
    low = part - high
    return [[wide(half[i : i + 1]) for i in range(4)] for half in (high, low)]


def fill(block_row, groups, count, parts, stores):
    block = wide(block_row)
    for group, use_here, use_there in groups:
        here = block == jnp.bfloat16(group)
        there = block == jnp.bfloat16((group - 1) % count)
        for (part_here, part_there), store in zip(parts, stores):
            value = jnp.where(there, part_there, 0.0) if use_there else 0.0
            value = jnp.where(here, part_here, value) if use_here else value
            store(group, value.astype(jnp.bfloat16))


def store_in(table, top):
    def store(group, value):
        table[pl.ds(top + 16 * group, 16), :] = value

    return store


def build_cols(geom, table_hi, table_lo):
    inside = TC // 16
    count = WIN // 16
    groups = [(group, True, True) for group in range(inside)]
    groups += [(inside, False, True), (count - 1, True, False)]
    parts = patterns(geom[17:18], split_rows(geom[8:12]))
    fill(geom[16:17], groups, count, parts, (store_in(table_hi, 0), store_in(table_lo, 0)))


def build_rows(geom, vector, fold, table_hi, table_lo):
    first, second = vector[0:1], vector[1:2]
    real = first * geom[0:4] + second * geom[4:8]
    imag = second * geom[0:4] - first * geom[4:8]
    count = fold // 16
    parts = patterns(geom[13:14], split_rows(real) + split_rows(imag))
    stores = [store_in(table, top) for top in (0, fold) for table in (table_hi, table_lo)]
    fill(geom[12:13], [(group, True, True) for group in range(count)], count, parts, stores)


def place_all(chunks, offsets, block_at, tiles, slabs):
    cap = chunks.shape[3]
    step = math.gcd(slabs, 8)

    def some(count, carry):
        tile = count // (slabs // step)
        first = (count - tile * (slabs // step)) * step
        spots, turned = [], []
        for which in range(step):
            offset = offsets[(first + which) * tiles + tile]
            chunk = offset // cap
            shift = offset - chunk * cap
            spots.append((chunk, shift))
            turned.append(pltpu.roll(block_at(first + which, tile), shift, 1))
        lane = lax.broadcasted_iota(jnp.int32, turned[0].shape, 1)
        for (chunk, shift), block in zip(spots, turned):
            chunks[tile, chunk] = jnp.where(lane >= shift, block, chunks[tile, chunk])
            chunks[tile, chunk + 1] = jnp.where(lane < shift, block, 0.0)
        return carry

    lax.fori_loop(0, tiles * (slabs // step), some, 0)


def fetch_all(chunks, offsets, out_ref, tiles, slabs):
    cap = chunks.shape[3]
    step = math.gcd(slabs, 8)

    def some(count, carry):
        tile = count // (slabs // step)
        first = (count - tile * (slabs // step)) * step
        lane = lax.broadcasted_iota(jnp.int32, chunks.shape[2:], 1)
        turned = []
        for which in range(step):
            offset = offsets[(first + which) * tiles + tile]
            chunk = offset // cap
            shift = offset - chunk * cap
            both = jnp.where(lane >= shift, chunks[tile, chunk], chunks[tile, chunk + 1])
            turned.append(pltpu.roll(both, lax.rem(cap - shift, cap), 1))
        for which in range(step):
            out_ref[(first + which) * tiles + tile] = turned[which]
        return carry

    lax.fori_loop(0, tiles * (slabs // step), some, 0)


def circle(index):
    quarter = G // 4
    turn = (index + quarter // 2) // quarter
    x = (index - turn * quarter).astype(jnp.float32) * (2.0 * math.pi / G)
    y = x * x
    sin_x = 1.0 / 362880.0
    for term in (-1.0 / 5040.0, 1.0 / 120.0, -1.0 / 6.0, 1.0):
        sin_x = sin_x * y + term
    sin_x = sin_x * x
    cos_x = -1.0 / 3628800.0
    for term in (1.0 / 40320.0, -1.0 / 720.0, 1.0 / 24.0, -0.5, 1.0):
        cos_x = cos_x * y + term
    odd = (turn & 1) == 1
    cos_out = jnp.where(odd, sin_x, cos_x)
    sin_out = jnp.where(odd, cos_x, sin_x)
    cos_out = jnp.where(((turn + 1) & 2) == 2, -cos_out, cos_out)
    sin_out = jnp.where((turn & 2) == 2, -sin_out, sin_out)
    return cos_out, sin_out


def prepare_kernel(offsets, used, own, raw_ref, geom_ref, chunks):
    tiles, depth, _, cap = chunks.shape
    slabs = raw_ref.shape[0]
    fold = G // slabs
    chunks[...] = jnp.zeros(chunks.shape, jnp.float32)
    geom_ref[...] = jnp.zeros(geom_ref.shape, jnp.float32)
    place_all(chunks, offsets, lambda slab, tile: raw_ref[slab, tile], tiles, slabs)
    mine = own[0]
    steps = [circle((jnp.full((1, cap), tap, jnp.int32) * mine) & (G - 1)) for tap in range(1, 4)]

    def per_tile(tile, carry):
        def per_chunk(chunk, inner):
            raw = chunks[tile, chunk]
            row = jnp.maximum(raw[0:1].astype(jnp.int32), 0) + (G - 1)
            col = raw[1:2].astype(jnp.int32) + (WIN - 1)
            row_weights = cubic_weights(raw[2:3])
            col_weights = cubic_weights(raw[3:4])
            base_cos, base_sin = circle((row * mine) & (G - 1))
            for tap in range(4):
                cos_t, sin_t = base_cos, base_sin
                if tap:
                    step_cos, step_sin = steps[tap - 1]
                    cos_t = base_cos * step_cos - base_sin * step_sin
                    sin_t = base_sin * step_cos + base_cos * step_sin
                values = (row_weights[tap] * cos_t, row_weights[tap] * sin_t, col_weights[tap])
                for kind, value in enumerate(values):
                    at = 4 * kind + tap
                    geom_ref[tile, chunk, at : at + 1, :] = value
            row, col = row & (fold - 1), col & (WIN - 1)
            places = (row >> 4, row & 15, row >> 3, row & 7, col >> 4, col & 15)
            for kind, value in enumerate(places):
                at = 12 + kind
                geom_ref[tile, chunk, at : at + 1, :] = value.astype(jnp.float32)
            return inner

        lax.fori_loop(0, used[tile], per_chunk, 0)
        return carry

    lax.fori_loop(0, tiles, per_tile, 0)


def spread_kernel(offsets, used, geom_ref, vec_ref, field_ref, chunks, acc, rows0, cols0, rows1, cols1):
    tiles, fold2, _ = field_ref.shape
    slabs = vec_ref.shape[0] // tiles
    fold = fold2 // 2
    cap = chunks.shape[3]
    for table in (cols0, cols1):
        table[...] = jnp.zeros(table.shape, table.dtype)
    field_ref[...] = jnp.zeros(field_ref.shape, jnp.float32)
    chunks[...] = jnp.zeros(chunks.shape, jnp.float32)
    place_all(chunks, offsets, lambda slab, tile: vec_ref[slab * tiles + tile], tiles, slabs)
    sets = ((rows0, cols0), (rows1, cols1))

    def build(which, tile, chunk):
        rows, cols = sets[which]
        geom = geom_ref[tile, chunk]
        build_rows(geom, chunks[tile, chunk], fold, rows.at[0], rows.at[1])
        build_cols(geom, cols.at[0], cols.at[1])

    def add(which):
        rows, cols = sets[which]
        left = jnp.concatenate([rows[0], rows[1], rows[0]], axis=1)
        right = jnp.concatenate([cols[0], cols[0], cols[1]], axis=1)
        acc[...] += dot_f32(left, right, ((1,), (1,)))

    build(0, 0, 0)

    def per_tile(tile, carry):
        acc[...] = jnp.zeros(acc.shape, jnp.float32)
        behind = jnp.minimum(tile + 1, tiles - 1)

        def per_pair(pair, inner):
            more = 2 * pair + 2 < used[tile]
            add(0)
            build(1, tile, 2 * pair + 1)
            add(1)
            build(0, jnp.where(more, tile, behind), jnp.where(more, 2 * pair + 2, 0))
            return inner

        lax.fori_loop(0, used[tile] // 2, per_pair, 0)

        @pl.when(lax.rem(used[tile], 2) == 1)
        def _():
            add(0)
            build(0, behind, 0)

        lane = lax.broadcasted_iota(jnp.int32, (fold2, TC), 1)
        rim = acc[:, TC:]
        field_ref[tile] += acc[:, :TC]
        after = lax.rem(tile + 1, tiles)
        before = lax.rem(tile + tiles - 1, tiles)
        field_ref[after] += jnp.where(lane < TC // 2, rim, 0.0)
        field_ref[before] += jnp.where(lane < TC // 2, 0.0, rim)
        return carry

    lax.fori_loop(0, tiles, per_tile, 0)


def smooth_kernel(
    offsets, used, geom_ref, field_ref, spec_ref, row_fwd, row_inv, col_fwd, col_inv,
    turn_cos, turn_sin, mix_cos, mix_sin, out_ref, work, whi, wlo, cols0, cols1, chunks, blend0, blend1,
):
    tiles, fold2, _ = field_ref.shape
    fold = fold2 // 2
    slabs = out_ref.shape[0] // tiles
    cap = geom_ref.shape[3]

    half = fold // 2
    many = math.gcd(tiles, 4)

    def product_rows(matrix, columns):
        high, low = halves(jnp.concatenate(columns, axis=1))
        result = dot_f32(matrix[...], jnp.concatenate([high, low, high], axis=0), ((1,), (0,)))
        return [result[:, TC * i : TC * (i + 1)] for i in range(len(columns))]

    def rows_forward(group, carry):
        columns = []
        for which in range(many):
            block = field_ref[many * group + which]
            real_a, real_b = block[:half], block[half:fold]
            imag_a, imag_b = block[fold : fold + half], block[fold + half :]
            real_d, imag_d = real_a - real_b, imag_a - imag_b
            columns.append(jnp.concatenate([real_a + real_b, imag_a + imag_b], axis=0))
            columns.append(
                jnp.concatenate(
                    [
                        real_d * mix_cos[...] + imag_d * mix_sin[...],
                        imag_d * mix_cos[...] - real_d * mix_sin[...],
                    ],
                    axis=0,
                )
            )
        results = product_rows(row_fwd, columns)
        for which in range(many):
            for odd in range(2):
                result = results[2 * which + odd]
                at = odd * half
                work[many * group + which, at : at + half, :] = result[:half]
                work[many * group + which, fold + at : fold + at + half, :] = result[half:]
        return carry

    def rows_inverse(group, carry):
        columns = []
        for which in range(many):
            block = work[many * group + which]
            columns.append(jnp.concatenate([block[:half], block[fold : fold + half]], axis=0))
            columns.append(jnp.concatenate([block[half:fold], block[fold + half :]], axis=0))
        results = product_rows(row_inv, columns)
        for which in range(many):
            even, odd = results[2 * which], results[2 * which + 1]
            real_t = odd[:half] * mix_cos[...] - odd[half:] * mix_sin[...]
            imag_t = odd[:half] * mix_sin[...] + odd[half:] * mix_cos[...]
            at = many * group + which
            work[at, :half, :] = even[:half] + real_t
            work[at, half:fold, :] = even[:half] - real_t
            work[at, fold : fold + half, :] = even[half:] + imag_t
            work[at, fold + half :, :] = even[half:] - imag_t
        return carry

    def tile_pass(sign):
        def step(group, carry):
            top = pl.multiple_of(8 * group, 8)
            real_at, imag_at = pl.ds(top, 8), pl.ds(fold + top, 8)
            real = [work[t, real_at, :] for t in range(tiles)]
            imag = [work[t, imag_at, :] for t in range(tiles)]

            def turned(real, imag):
                out_r, out_i = [], []
                for t in range(tiles):
                    cos_t, sin_t = turn_cos[t : t + 1, :], sign * turn_sin[t : t + 1, :]
                    out_r.append(real[t] * cos_t - imag[t] * sin_t)
                    out_i.append(real[t] * sin_t + imag[t] * cos_t)
                return out_r, out_i

            if sign < 0:
                real, imag = turned(*fft_list(real, imag, sign))
            else:
                real, imag = fft_list(*turned(real, imag), sign)
            for t in range(tiles):
                work[t, real_at, :] = real[t]
                work[t, imag_at, :] = imag[t]
            return carry

        lax.fori_loop(0, fold // 8, step, 0)

    def lane_pass():
        def product(left, matrix):
            high, low = halves(left)
            return dot_f32(jnp.concatenate([high, low, high], axis=1), matrix[...], ((1,), (0,)))

        def step(group, carry):
            ats = [many * group + which for which in range(many)]
            left = jnp.concatenate(
                [jnp.concatenate([work[at, :fold, :], work[at, fold:, :]], axis=1) for at in ats], axis=0
            )
            middle = product(left, col_fwd)
            spec = jnp.concatenate([spec_ref[at].T for at in ats], axis=0)
            middle = middle * jnp.concatenate([spec, spec], axis=1)
            result = product(middle, col_inv)
            for which, at in enumerate(ats):
                part = result[fold * which : fold * (which + 1)]
                work[at, :fold, :] = part[:, :TC]
                work[at, fold:, :] = part[:, TC:]
            return carry

        lax.fori_loop(0, tiles // many, step, 0)

    lax.fori_loop(0, tiles // many, rows_forward, 0)
    tile_pass(-1.0)
    lane_pass()
    tile_pass(1.0)
    lax.fori_loop(0, tiles // many, rows_inverse, 0)

    sets = ((cols0, blend0), (cols1, blend1))
    blend1[...] = jnp.zeros(blend1.shape, jnp.float32)
    for table in (cols0, cols1):
        table[...] = jnp.zeros(table.shape, table.dtype)
    chunks[...] = jnp.zeros(chunks.shape, jnp.float32)

    def gathered(geom, blend):
        block = jnp.broadcast_to(geom[14:15], (8, cap))
        count = fold // 8
        zero = jnp.zeros((8, cap), jnp.float32)
        here = [zero, zero]
        there = [zero, zero]
        for group in range(count):
            hit = block == float(group)
            for part in range(2):
                top = part * fold + 8 * group
                after = part * fold + 8 * ((group + 1) % count)
                here[part] = jnp.where(hit, blend[top : top + 8, :], here[part])
                there[part] = jnp.where(hit, blend[after : after + 8, :], there[part])
        position = lax.broadcasted_iota(jnp.int32, (8, cap), 0).astype(jnp.float32)
        first, second = zero, zero
        for shift, (real, imag) in ((0.0, here), (8.0, there)):
            hits = [position == geom[15:16] + (tap - shift) for tap in range(4)]
            cos_t = pick(hits, [jnp.broadcast_to(geom[i : i + 1], (8, cap)) for i in range(4)])
            sin_t = pick(hits, [jnp.broadcast_to(geom[4 + i : 5 + i], (8, cap)) for i in range(4)])
            first = first + cos_t * real - sin_t * imag
            second = second + cos_t * imag + sin_t * real
        return jnp.sum(first, axis=0, keepdims=True), jnp.sum(second, axis=0, keepdims=True)

    spare = chunks.shape[1] - 1

    def start_blend(which, tile, chunk):
        cols, blend = sets[which]
        build_cols(geom_ref[tile, chunk], cols.at[0], cols.at[1])
        left = jnp.concatenate([whi[...], wlo[...], whi[...]], axis=1)
        right = jnp.concatenate([cols[0], cols[0], cols[1]], axis=0)
        blend[...] = dot_f32(left, right, ((1,), (0,)))

    def finish(which, tile, chunk):
        first, second = gathered(geom_ref[tile, chunk], sets[which][1])
        chunks[tile, chunk, 0:1, :] = first
        chunks[tile, chunk, 1:2, :] = second

    def per_tile(tile, last):
        lane = lax.broadcasted_iota(jnp.int32, (fold2, TC), 1)
        after = lax.rem(tile + 1, tiles)
        before = lax.rem(tile + tiles - 1, tiles)
        rim = jnp.where(lane < TC // 2, work[after], work[before])
        high, low = halves(jnp.concatenate([work[tile], rim], axis=1))
        whi[...] = high
        wlo[...] = low

        def per_pair(pair, last):
            start_blend(0, tile, 2 * pair)
            finish(1, *last)
            start_blend(1, tile, 2 * pair + 1)
            finish(0, tile, 2 * pair)
            return tile, 2 * pair + 1

        last = lax.fori_loop(0, used[tile] // 2, per_pair, last)
        odd = lax.rem(used[tile], 2) == 1

        @pl.when(odd)
        def _():
            start_blend(0, tile, used[tile] - 1)
            finish(1, *last)
            finish(0, tile, used[tile] - 1)

        return jnp.where(odd, 0, last[0]), jnp.where(odd, spare, last[1])

    finish(1, *lax.fori_loop(0, tiles, per_tile, (0, spare)))
    fetch_all(chunks, offsets, out_ref, tiles, slabs)


def call_kernel(kernel, shape, scratch, scalars, args):
    vmem = pl.BlockSpec(memory_space=pltpu.VMEM)
    smem = pl.BlockSpec(memory_space=pltpu.SMEM)
    return pl.pallas_call(
        kernel,
        out_shape=jax.ShapeDtypeStruct(shape, jnp.float32),
        in_specs=[smem] * len(scalars) + [vmem] * len(args),
        out_specs=vmem,
        scratch_shapes=scratch,
        compiler_params=pltpu.CompilerParams(vmem_limit_bytes=VMEM_BYTES),
        cost_estimate=pl.CostEstimate(flops=4 * 10**9, bytes_accessed=10**7, transcendentals=0),
    )(*scalars, *args)


def shared(value):
    count = lax.axis_size("slab")
    copies = jnp.broadcast_to(value[None], (count,) + value.shape)
    return lax.all_to_all(copies, "slab", 0, 0, tiled=True)


def spectrum_slab(spectrum, fold):
    slabs = G // fold
    pieces = spectrum.reshape(fold // 2, 2, slabs, -1).transpose(2, 3, 1, 0) * (1.0 / (G * G))
    pieces = pieces.reshape(slabs, -1, fold)
    return lax.all_to_all(pieces, "slab", 0, 0, tiled=True)


def spectrum_rows(mine, tiles, fold):
    count = lax.axis_size("rhs")
    copies = jnp.broadcast_to(mine[None], (count,) + mine.shape)
    every = lax.all_to_all(copies, "rhs", 0, 0, tiled=True)
    columns = every.transpose(1, 0, 2, 3).reshape(G // tiles, tiles, fold)
    return columns.transpose(1, 0, 2)


def per_device(targets, counts, cell_rows, cell_cols, fractions, spectrum, noise_var):
    tiles, cap = cell_rows.shape
    slabs = lax.axis_size("slab")
    fold = G // slabs
    slot_index = lax.broadcasted_iota(jnp.int32, (tiles, cap), 1)
    live = (slot_index < counts[:, None]).astype(jnp.float32)[:, None, :]
    noise = noise_var[0]
    start = live * targets.transpose(1, 0, 2)

    own = lax.axis_index("slab").astype(jnp.int32).reshape(1)
    rows = jnp.where(live > 0, (own[0] * fold + cell_rows).astype(jnp.float32)[:, None], -1.0)
    payload = jnp.concatenate(
        [rows, cell_cols.astype(jnp.float32)[:, None], fractions.transpose(1, 0, 2), start], axis=1
    )
    every = shared(payload.reshape(-1, cap)).reshape((slabs,) + payload.shape)
    every, spectrum = lax.optimization_barrier((every, spectrum))
    start_all = every[:, :, 4:6].reshape(slabs * tiles, 2, cap)
    filled = jnp.sum((every[:, :, 0] >= 0.0).astype(jnp.int32), axis=2)
    before = [jnp.zeros((tiles,), jnp.int32)]
    for slab in range(slabs):
        before.append(before[-1] + filled[slab])
    offsets = jnp.concatenate(before[:-1])
    used = (before[-1] + (cap - 1)) // cap
    depth = slabs + 2
    geom = call_kernel(
        prepare_kernel,
        (tiles, depth, GEOM_ROWS, cap),
        [pltpu.VMEM((tiles, depth, every.shape[2], cap), jnp.float32)],
        (offsets, used, own),
        (every,),
    )
    mine = spectrum_slab(spectrum, fold)
    geom, mine = lax.optimization_barrier((geom, mine))
    spec = spectrum_rows(mine, tiles, fold)
    row_fwd, row_inv = [jnp.asarray(m) for m in row_matrices(fold // 2)]
    col_fwd, col_inv = [jnp.asarray(m) for m in col_matrices(TC)]
    mix_cos, mix_sin = [
        jnp.asarray(np.repeat(t[:, 1:2], TC, axis=1).astype(np.float32)) for t in angle_tables(fold // 2, 2, fold)
    ]
    turn_cos, turn_sin = [jnp.asarray(t.astype(np.float32)) for t in angle_tables(tiles, TC, G)]

    def vmem(shape, dtype):
        return pltpu.VMEM(shape, dtype)

    half = jnp.bfloat16
    row_table = vmem((2, 2 * fold, cap), half)
    col_table = vmem((2, WIN, cap), half)
    point_chunks = vmem((tiles, depth, 2, cap), jnp.float32)

    def partial_product(vector):
        field = call_kernel(
            spread_kernel,
            (tiles, 2 * fold, TC),
            [point_chunks, vmem((2 * fold, WIN), jnp.float32)] + [row_table, col_table] * 2,
            (offsets, used),
            (geom, vector),
        )
        return call_kernel(
            smooth_kernel,
            (slabs * tiles, 2, cap),
            [vmem((tiles, 2 * fold, TC), jnp.float32)]
            + [vmem((2 * fold, WIN), half)] * 2
            + [col_table] * 2
            + [point_chunks]
            + [vmem((2 * fold, cap), jnp.float32)] * 2,
            (offsets, used),
            (geom, field, spec, row_fwd, row_inv, col_fwd, col_inv, turn_cos, turn_sin, mix_cos, mix_sin),
        )

    def total(value):
        return jnp.sum(value, axis=(0, 2))

    def per_rhs(scale):
        return scale[None, :, None]

    direction_all = start_all
    residual_all = start_all
    direction = start
    residual = start
    solution = jnp.zeros_like(start)
    norm_now = total(start_all * start_all)
    for repeat in range(ITERS):
        partial = partial_product(direction_all)
        blocks = partial.reshape(slabs, tiles, 2, cap)
        if repeat + 1 < ITERS:
            smoothed = jnp.sum(lax.all_to_all(blocks, "slab", 0, 0, tiled=True), axis=0)
            image = live * smoothed + noise * direction
            image_all = shared(image).reshape(slabs * tiles, 2, cap)
            alpha = norm_now / total(direction_all * image_all)
            residual_all = residual_all - per_rhs(alpha) * image_all
            norm_next = total(residual_all * residual_all)
            beta = norm_next / norm_now
            solution = solution + per_rhs(alpha) * direction
            residual = residual - per_rhs(alpha) * image
            direction = residual + per_rhs(beta) * direction
            direction_all = residual_all + per_rhs(beta) * direction_all
            norm_now = norm_next
        else:
            share = total(direction_all * partial)
            extra = jnp.broadcast_to(share[None, None, :, None], (slabs, 1, 2, cap))
            blocks = jnp.concatenate([blocks, extra], axis=1)
            summed = jnp.sum(lax.all_to_all(blocks, "slab", 0, 0, tiled=True), axis=0)
            image = live * summed[:tiles] + noise * direction
            product = summed[tiles, :, 0] + noise * total(direction_all * direction_all)
            alpha = norm_now / product
            solution = solution + per_rhs(alpha) * direction
            residual = residual - per_rhs(alpha) * image
    return solution.transpose(1, 0, 2), residual.transpose(1, 0, 2)


def solution(mesh):
    placed = (
        P("rhs", "slab", None),
        P("slab"),
        P("slab", None),
        P("slab", None),
        P(None, "slab", None),
        P(None, ("slab", "rhs")),
        P(),
    )
    return jax.shard_map(
        per_device,
        mesh=mesh,
        in_specs=placed,
        out_specs=(P("rhs", "slab", None), P("rhs", "slab", None)),
        check_vma=False,
    )
```

profile of v0, /device:TPU:0, one launch (start us, length us, event | category | flops | bytes accessed | tf_op | source)
XLA Modules:
  0.0 282.9 jit_solution(17895208686861420805)
XLA Ops:
  0.6 0.7 fusion.11
  1.4 0.7 convert_bitcast_fusion
  2.1 0.8 select_bitcast_fusion
  2.9 0.8 multiply_bitcast_fusion
  3.6 0.8 pad_maximum_fusion.1
  4.6 27.4 %all_to_all.30 = f32[8,96,256]{2,1,0:T(8,128)S(1)} all-to-all(f32[8,96,256]{2,1,0:T(8,128)S(1)} %broadcast_in_dim.19), channel_id=1, replica_groups=mesh['slab'=8,'rhs'=4] {'slab'}, dimensions={0} | all-to-all | bytes 1572864 | tf_op jit(solution)/shard_map/all_to_all | solution.py:522
  31.9 0.5 copy.104
  32.5 0.3 copy.106
  32.8 0.5 copy.107
  33.3 1.3 reshape.79
  34.6 3.6 %all-to-all-start.1 = ((f32[8,64,256]{2,1,0:T(8,128)}), f32[8,64,256]{2,1,0:T(8,128)S(1)}, u32[]{:S(2)}, u32[]{:S(2)}) async-start(f32[8,64,256]{2,1,0:T(8,128)} %reshape.79), calls=%async_computation.1 | async-start | bytes 1048576 | tf_op jit(solution)/shard_map/all_to_all | solution.py:529
  38.1 0.3 copy.105.raw_ref
  38.4 0.3 convert_reduce_fusion
  38.8 0.3 slice_reduce_fusion
  39.2 7.9 %shard_map.158.geom_ref = f32[16,10,24,256]{3,2,1,0:T(8,128)S(1)} custom-call(s32[128]{0:T(128)S(1)} %concatenate.10.offsets, s32[16]{0:T(128)S(1)} %get-tuple-element.30.used, s32[1]{0:T(128)} %bitcast.5.own, f32[8,16,6,256]{3,2,1,0:T(8,128)S(1)} %copy.105.raw_ref), custom_call_target="tpu_custom_call" | custom-call | flops 4000000000 | bytes 10000000 | tf_op jit(solution)/shard_map/pallas_call | solution.py:508
  47.1 1.9 copy-done.14
  48.9 3.4 %all-to-all-done.1 = f32[8,64,256]{2,1,0:T(8,128)S(1)} async-done(((f32[8,64,256]{2,1,0:T(8,128)}), f32[8,64,256]{2,1,0:T(8,128)S(1)}, u32[]{:S(2)}, u32[]{:S(2)}) %all-to-all-start.1) | async-done | bytes 524320 | tf_op jit(solution)/shard_map/all_to_all | solution.py:529
  52.3 1.6 broadcast_in_dim.20
  54.0 3.6 %all-to-all-start.2 = ((f32[4,8,64,256]{3,2,1,0:T(8,128)}), f32[4,8,64,256]{3,2,1,0:T(8,128)S(1)}, u32[]{:S(2)}, u32[]{:S(2)}) async-start(f32[4,8,64,256]{3,2,1,0:T(8,128)} %broadcast_in_dim.20), calls=%async_computation.2 | async-start | bytes 4194304 | tf_op jit(solution)/shard_map/all_to_all | solution.py:535
  57.6 0.1 copy.108
  57.8 2.1 copy-done.15
  59.9 34.7 %shard_map.159.field_ref = f32[16,512,128]{2,1,0:T(8,128)S(1)} custom-call(s32[128]{0:T(128)S(1)} %concatenate.10.offsets, s32[16]{0:T(128)S(1)} %get-tuple-element.30.used, f32[16,10,24,256]{3,2,1,0:T(8,128)S(1)} %copy-done.15, f32[128,2,256]{2,1,0:T(2,128)S(1)} %bitcast.59), custom_call_target="tpu_custom_call" | custom-call | flops 4000000000 | bytes 10000000 | tf_op jit(solution)/shard_map/pallas_call | solution.py:508
  94.6 1.9 copy-done.12
  96.7 1.2 copy.142
  98.0 0.7 copy-done.13
  99.2 2.1 copy-done.16
  101.3 48.6 %shard_map.160 = f32[128,2,256]{2,1,0:T(2,128)} custom-call(s32[128]{0:T(128)S(1)} %concatenate.10.offsets, s32[16]{0:T(128)S(1)} %get-tuple-element.30.used, f32[16,10,24,256]{3,2,1,0:T(8,128)S(1)} %copy-done.16, f32[16,512,128]{2,1,0:T(8,128)S(1)} %copy-done.13, f32[16,128,256]{2,1,0:T(8,128)S(1)} %bitcast.56, bf16[256,768]{1,0:T(8,128)(2,1)S(1)} %copy-done.3, ...), custom_call_target="tpu_custom_call" | custom-call | flops 4000000000 | bytes 10000000 | tf_op jit(solution)/shard_map/pallas_call | solution.py:508
  149.9 4.0 %all-to-all-start.3 = ((f32[8,16,2,256]{3,2,1,0:T(2,128)}), f32[8,16,2,256]{3,2,1,0:T(2,128)}, u32[]{:S(2)}, u32[]{:S(2)}) async-start(f32[8,16,2,256]{3,2,1,0:T(2,128)} %bitcast.12), calls=%async_computation.3 | async-start | bytes 524288 | tf_op jit(solution)/shard_map/all_to_all | solution.py:625
  154.6 9.2 %all-to-all-done.3 = f32[8,16,2,256]{3,2,1,0:T(2,128)} async-done(((f32[8,16,2,256]{3,2,1,0:T(2,128)}), f32[8,16,2,256]{3,2,1,0:T(2,128)}, u32[]{:S(2)}, u32[]{:S(2)}) %all-to-all-start.3) | async-done | bytes 262176 | tf_op jit(solution)/shard_map/all_to_all | solution.py:625
  163.8 1.7 reduce_sum.76
  165.4 0.8 multiply_add_fusion
  166.4 12.5 %all_to_all.31 = f32[8,16,2,256]{3,2,1,0:T(2,128)S(1)} all-to-all(f32[8,16,2,256]{3,2,1,0:T(2,128)S(1)} %broadcast_in_dim.21), channel_id=1, replica_groups=mesh['slab'=8,'rhs'=4] {'slab'}, dimensions={0} | all-to-all | bytes 524288 | tf_op jit(solution)/shard_map/all_to_all | solution.py:522
  178.9 1.3 multiply_reduce_fusion.3
  180.2 1.2 multiply_reduce_fusion.2
  181.4 0.5 copy-done.29
  181.9 0.5 copy-done.27
  182.5 0.2 fusion.1.vec_ref
  182.7 2.1 copy-done.17
  184.8 34.7 %shard_map.161.field_ref = f32[16,512,128]{2,1,0:T(8,128)S(1)} custom-call(s32[128]{0:T(128)S(1)} %concatenate.10.offsets, s32[16]{0:T(128)S(1)} %get-tuple-element.30.used, f32[16,10,24,256]{3,2,1,0:T(8,128)S(1)} %copy-done.17, f32[128,2,256]{2,1,0:T(2,128)S(1)} %fusion.1.vec_ref), custom_call_target="tpu_custom_call" | custom-call | flops 4000000000 | bytes 10000000 | tf_op jit(solution)/shard_map/pallas_call | solution.py:508
  219.5 47.9 %shard_map.162 = f32[128,2,256]{2,1,0:T(2,128)S(1)} custom-call(s32[128]{0:T(128)S(1)} %concatenate.10.offsets, s32[16]{0:T(128)S(1)} %get-tuple-element.30.used, f32[16,10,24,256]{3,2,1,0:T(8,128)S(1)} %copy-done.17, f32[16,512,128]{2,1,0:T(8,128)S(1)} %shard_map.161.field_ref, f32[16,128,256]{2,1,0:T(8,128)S(1)} %bitcast.57, ...), custom_call_target="tpu_custom_call" | custom-call | flops 4000000000 | bytes 10000000 | tf_op jit(solution)/shard_map/pallas_call | solution.py:508
  267.5 0.4 multiply_reduce_fusion.1
  268.0 0.8 pad_maximum_fusion
  268.8 3.6 %all-to-all-start.5 = ((f32[8,17,2,256]{3,2,1,0:T(2,128)}), f32[8,17,2,256]{3,2,1,0:T(2,128)S(1)}, u32[]{:S(2)}, u32[]{:S(2)}) async-start(f32[8,17,2,256]{3,2,1,0:T(2,128)} %pad_maximum_fusion), calls=%async_computation.5 | async-start | bytes 557056 | tf_op jit(solution)/shard_map/all_to_all | solution.py:641
  272.4 0.7 copy.116
  273.1 1.3 multiply_reduce_fusion
  274.5 6.8 %all-to-all-done.5 = f32[8,17,2,256]{3,2,1,0:T(2,128)S(1)} async-done(((f32[8,17,2,256]{3,2,1,0:T(2,128)}), f32[8,17,2,256]{3,2,1,0:T(2,128)S(1)}, u32[]{:S(2)}, u32[]{:S(2)}) %all-to-all-start.5) | async-done | bytes 278560 | tf_op jit(solution)/shard_map/all_to_all | solution.py:641
  281.5 0.7 fusion.10
  282.2 0.7 fusion.5
  (72 shorter events, 1.5 us)
Async XLA Ops:
  1.4 3.2 %copy-start.20 = (f32[16,256]{1,0:T(8,128)}, f32[16,256]{1,0:T(8,128)S(1)}, u32[]{:S(2)}) copy-start(f32[16,256]{1,0:T(8,128)S(1)} %fusion.11) | copy-start | bytes 49156
  4.5 27.9 %copy-start.22 = (f32[2048,64]{0,1:T(8,128)S(1)}, f32[2048,64]{0,1:T(8,128)}, u32[]{:S(2)}) copy-start(f32[2048,64]{0,1:T(8,128)} %param.20) | copy-start | bytes 1572868
  32.4 25.2 %copy-start.18 = (f32[8,96,256]{2,0,1:T(8,128)}, f32[8,96,256]{2,0,1:T(8,128)S(1)}, u32[]{:S(2)}) copy-start(f32[8,96,256]{2,0,1:T(8,128)S(1)} %copy.104) | copy-start | bytes 2359300
  34.6 17.8 %all-to-all-start.1 = ((f32[8,64,256]{2,1,0:T(8,128)}), f32[8,64,256]{2,1,0:T(8,128)S(1)}, u32[]{:S(2)}, u32[]{:S(2)}) async-start(f32[8,64,256]{2,1,0:T(8,128)} %reshape.79), calls=%async_computation.1 | async-start | bytes 1048576 | tf_op jit(solution)/shard_map/all_to_all | solution.py:529
  47.1 1.9 copy-start.14
  54.0 42.5 %all-to-all-start.2 = ((f32[4,8,64,256]{3,2,1,0:T(8,128)}), f32[4,8,64,256]{3,2,1,0:T(8,128)S(1)}, u32[]{:S(2)}, u32[]{:S(2)}) async-start(f32[4,8,64,256]{3,2,1,0:T(8,128)} %broadcast_in_dim.20), calls=%async_computation.2 | async-start | bytes 4194304 | tf_op jit(solution)/shard_map/all_to_all | solution.py:535
  57.8 2.1 copy-start.15
  94.6 1.9 copy-start.12
  96.5 2.2 copy-start.13
  96.6 2.1 copy-start
  96.7 2.2 copy-start.1
  96.7 2.4 copy-start.2
  96.7 2.5 copy-start.3
  96.7 2.5 copy-start.5
  96.7 2.4 copy-start.7
  96.7 2.4 copy-start.9
  96.7 2.4 copy-start.10
  99.2 2.1 copy-start.16
  149.9 13.9 %all-to-all-start.3 = ((f32[8,16,2,256]{3,2,1,0:T(2,128)}), f32[8,16,2,256]{3,2,1,0:T(2,128)}, u32[]{:S(2)}, u32[]{:S(2)}) async-start(f32[8,16,2,256]{3,2,1,0:T(2,128)} %bitcast.12), calls=%async_computation.3 | async-start | bytes 524288 | tf_op jit(solution)/shard_map/all_to_all | solution.py:625
  178.9 3.1 %copy-start.19 = (f32[8,16,2,256]{3,2,1,0:T(2,128)}, f32[8,16,2,256]{3,2,1,0:T(2,128)S(1)}, u32[]{:S(2)}) copy-start(f32[8,16,2,256]{3,2,1,0:T(2,128)S(1)} %all_to_all.31) | copy-start | bytes 786436
  180.2 1.8 copy-start.25
  181.4 0.5 copy-start.29
  181.9 0.5 copy-start.27
  182.7 2.1 copy-start.17
  184.8 34.7 %copy-start.4 = (bf16[256,768]{1,0:T(8,128)(2,1)S(1)}, bf16[256,768]{1,0:T(8,128)(2,1)}, u32[]{:S(2)}) copy-start(bf16[256,768]{1,0:T(8,128)(2,1)} %constant.50.clone.row_fwd) | copy-start | bytes 1179652
  184.8 34.7 %copy-start.6 = (f32[128,128]{1,0:T(8,128)S(1)}, f32[128,128]{1,0:T(8,128)}, u32[]{:S(2)}) copy-start(f32[128,128]{1,0:T(8,128)} %constant.55.clone.mix_sin) | copy-start | bytes 196612
  184.8 34.7 %copy-start.8 = (f32[128,128]{1,0:T(8,128)S(1)}, f32[128,128]{1,0:T(8,128)}, u32[]{:S(2)}) copy-start(f32[128,128]{1,0:T(8,128)} %constant.54.clone.mix_cos) | copy-start | bytes 196612
  184.8 34.7 %copy-start.11 = (f32[16,128]{1,0:T(8,128)S(1)}, f32[16,128]{1,0:T(8,128)}, u32[]{:S(2)}) copy-start(f32[16,128]{1,0:T(8,128)} %constant.56.clone.turn_cos) | copy-start | bytes 24580
  267.5 14.0 %copy-start.21 = (f32[16,256]{1,0:T(8,128)S(1)}, f32[16,256]{1,0:T(8,128)}, u32[]{:S(2)}) copy-start(f32[16,256]{1,0:T(8,128)} %copy-done.20) | copy-start | bytes 49156
  267.5 14.0 %copy-start.23 = (f32[16,2,256]{2,1,0:T(2,128)S(1)}, f32[16,2,256]{2,1,0:T(2,128)}, u32[]{:S(2)}) copy-start(f32[16,2,256]{2,1,0:T(2,128)} %reduce_sum.76) | copy-start | bytes 98308
  267.5 14.0 %copy-start.24 = (f32[2,16,256]{2,1,0:T(8,128)S(1)}, f32[2,16,256]{2,1,0:T(8,128)}, u32[]{:S(2)}) copy-start(f32[2,16,256]{2,1,0:T(8,128)} %param.15) | copy-start | bytes 98308
  267.5 14.0 %copy-start.26 = (f32[2]{0:T(128)S(1)}, f32[2]{0:T(128)}, u32[]{:S(2)}) copy-start(f32[2]{0:T(128)} %copy-done.25) | copy-start | bytes 28
  267.5 14.0 %copy-start.28 = (f32[2]{0:T(128)S(1)}, f32[2]{0:T(128)}, u32[]{:S(2)}) copy-start(f32[2]{0:T(128)} %copy-done.27) | copy-start | bytes 28
  268.8 12.5 %all-to-all-start.5 = ((f32[8,17,2,256]{3,2,1,0:T(2,128)}), f32[8,17,2,256]{3,2,1,0:T(2,128)S(1)}, u32[]{:S(2)}, u32[]{:S(2)}) async-start(f32[8,17,2,256]{3,2,1,0:T(2,128)} %pad_maximum_fusion), calls=%async_computation.5 | async-start | bytes 557056 | tf_op jit(solution)/shard_map/all_to_all | solution.py:641
where the time goes:
time: 286 us; the launch traced here: 283 us
  Pallas kernels  174 us (61%)
  blocking collectives  39.9 us (14%)
  local copies, waits for them, and re-layouts  19.8 us (7%)
  waiting for transfers between devices  19.4 us (7%)
  starting transfers between devices  14.8 us (5%)
  other arithmetic  13.5 us (5%)
    pallas_call x5, Pallas kernels, call_kernel(): pl.pallas_call(kernel, out_shape=jax.ShapeDtypeStruct(shape, jnp.float32)...  174 us
    all_to_all x2, blocking collectives, shared(): return lax.all_to_all(copies, 'slab', 0, 0, tiled=True)  39.9 us
    unnamed x60, local copies, waits for them, and re-layouts  12.4 us
    all_to_all x1, waiting for transfers between devices, per_device(): smoothed = jnp.sum(lax.all_to_all(blocks, 'slab', 0, 0, tiled=True), axis=0)  9.18 us
    all_to_all x1, waiting for transfers between devices, per_device(): summed = jnp.sum(lax.all_to_all(blocks, 'slab', 0, 0, tiled=True), axis=0)  6.8 us
  transfers between devices with their start and end apart: 4, of which 3 were waited for; matrix products, arithmetic and copies ran while one was open for 1% of the time, Pallas kernels for 15%

commit v1 on v0

--- a/solution.py
+++ b/solution.py
@@ -14,7 +14,7 @@
 ITERS = 2
 WIN = 2 * TC
 GEOM_ROWS = 24
-VMEM_BYTES = 30 * 1024 * 1024
+VMEM_SPARE = 2 * 1024 * 1024
 
 
 def cubic_weights(fraction):
@@ -294,7 +294,15 @@
             build(0, jnp.where(more, tile, behind), jnp.where(more, 2 * pair + 2, 0))
             return inner
 
-        lax.fori_loop(0, used[tile] // 2, per_pair, 0)
+        def per_four(four, inner):
+            return per_pair(2 * four + 1, per_pair(2 * four, inner))
+
+        fours = used[tile] // 4
+        lax.fori_loop(0, fours, per_four, 0)
+
+        @pl.when(used[tile] // 2 > 2 * fours)
+        def _():
+            per_pair(2 * fours, 0)
 
         @pl.when(lax.rem(used[tile], 2) == 1)
         def _():
@@ -487,7 +495,19 @@
             finish(0, tile, 2 * pair)
             return tile, 2 * pair + 1
 
-        last = lax.fori_loop(0, used[tile] // 2, per_pair, last)
+        def per_four(four, last):
+            return per_pair(2 * four + 1, per_pair(2 * four, last))
+
+        fours = used[tile] // 4
+        last = lax.fori_loop(0, fours, per_four, last)
+        pair = used[tile] // 2 > 2 * fours
+        before_pair = last
+
+        @pl.when(pair)
+        def _():
+            per_pair(2 * fours, before_pair)
+
+        last = (jnp.where(pair, tile, last[0]), jnp.where(pair, 4 * fours + 1, last[1]))
         odd = lax.rem(used[tile], 2) == 1
 
         @pl.when(odd)
@@ -505,13 +525,16 @@
 def call_kernel(kernel, shape, scratch, scalars, args):
     vmem = pl.BlockSpec(memory_space=pltpu.VMEM)
     smem = pl.BlockSpec(memory_space=pltpu.SMEM)
+    arrays = [(a.shape, a.dtype) for a in args] + [(shape, jnp.float32)]
+    arrays += [(part.shape, part.dtype) for part in scratch]
+    held = sum(math.prod(dims) * jnp.dtype(kind).itemsize for dims, kind in arrays)
     return pl.pallas_call(
         kernel,
         out_shape=jax.ShapeDtypeStruct(shape, jnp.float32),
         in_specs=[smem] * len(scalars) + [vmem] * len(args),
         out_specs=vmem,
         scratch_shapes=scratch,
-        compiler_params=pltpu.CompilerParams(vmem_limit_bytes=VMEM_BYTES),
+        compiler_params=pltpu.CompilerParams(vmem_limit_bytes=held + held // 4 + VMEM_SPARE),
         cost_estimate=pl.CostEstimate(flops=4 * 10**9, bytes_accessed=10**7, transcendentals=0),
     )(*scalars, *args)
 
@@ -522,11 +545,10 @@
     return lax.all_to_all(copies, "slab", 0, 0, tiled=True)
 
 
-def spectrum_slab(spectrum, fold):
+def spectrum_pieces(spectrum, fold):
     slabs = G // fold
     pieces = spectrum.reshape(fold // 2, 2, slabs, -1).transpose(2, 3, 1, 0) * (1.0 / (G * G))
-    pieces = pieces.reshape(slabs, -1, fold)
-    return lax.all_to_all(pieces, "slab", 0, 0, tiled=True)
+    return pieces.reshape(slabs, -1, fold)
 
 
 def spectrum_rows(mine, tiles, fold):
@@ -552,7 +574,7 @@
         [rows, cell_cols.astype(jnp.float32)[:, None], fractions.transpose(1, 0, 2), start], axis=1
     )
     every = shared(payload.reshape(-1, cap)).reshape((slabs,) + payload.shape)
-    every, spectrum = lax.optimization_barrier((every, spectrum))
+    every, pieces = lax.optimization_barrier((every, spectrum_pieces(spectrum, fold)))
     start_all = every[:, :, 4:6].reshape(slabs * tiles, 2, cap)
     filled = jnp.sum((every[:, :, 0] >= 0.0).astype(jnp.int32), axis=2)
     before = [jnp.zeros((tiles,), jnp.int32)]
@@ -568,7 +590,7 @@
         (offsets, used, own),
         (every,),
     )
-    mine = spectrum_slab(spectrum, fold)
+    mine = lax.all_to_all(pieces, "slab", 0, 0, tiled=True)
     geom, mine = lax.optimization_barrier((geom, mine))
     spec = spectrum_rows(mine, tiles, fold)
     row_fwd, row_inv = [jnp.asarray(m) for m in row_matrices(fold // 2)]

time: 286 us -> 274 us (0.958); the launches traced: 283 us -> 274 us
  blocking collectives: 39.9 us -> 12.5 us
  waiting for transfers between devices: 19.4 us -> 37.8 us
  Pallas kernels: 174 us -> 165 us
  starting transfers between devices: 14.8 us -> 22.3 us
    all_to_all x2 -> x1, blocking collectives: 39.9 us -> 12.5 us  [shared(): return lax.all_to_all(copies, 'slab', 0, 0, tiled=True)]
    all_to_all x1 -> x2, waiting for transfers between devices: 3.38 us -> 22 us  [the longest x1 18 us: shared(): return lax.all_to_all(copies, 'slab', 0, 0, tiled=True)]
    pallas_call x5, Pallas kernels: 174 us -> 165 us  [call_kernel(): pl.pallas_call(kernel, out_shape=jax.ShapeDtypeStruct(shape, jnp.float32)...]
    all_to_all x1 -> x2, starting transfers between devices: 3.59 us -> 10.9 us  [the longest x1 7.28 us: shared(): return lax.all_to_all(copies, 'slab', 0, 0, tiled=True)]
  transfers between devices with their start and end apart: 4 -> 5, of which waited for: 3 -> 4; matrix products, arithmetic and copies ran while one was open for 1% -> 2% of each run, Pallas kernels for 15% -> 14%
where the time goes in v1:
time: 274 us
  Pallas kernels  165 us (60%)
  waiting for transfers between devices  37.8 us (14%)
  starting transfers between devices  22.3 us (8%)
  local copies, waits for them, and re-layouts  20.7 us (8%)
  other arithmetic  13.6 us (5%)
  blocking collectives  12.5 us (5%)
    pallas_call x5, Pallas kernels, call_kernel(): pl.pallas_call(kernel, out_shape=jax.ShapeDtypeStruct(shape, jnp.float32)...  165 us
    all_to_all x1, waiting for transfers between devices, shared(): return lax.all_to_all(copies, 'slab', 0, 0, tiled=True)  18 us
    all_to_all x1, blocking collectives, shared(): return lax.all_to_all(copies, 'slab', 0, 0, tiled=True)  12.5 us
    unnamed x60, local copies, waits for them, and re-layouts  12.4 us
    all_to_all x1, waiting for transfers between devices, per_device(): smoothed = jnp.sum(lax.all_to_all(blocks, 'slab', 0, 0, tiled=True), axis=0)  9.01 us
    all_to_all x1, starting transfers between devices, shared(): return lax.all_to_all(copies, 'slab', 0, 0, tiled=True)  7.28 us
    all_to_all x1, waiting for transfers between devices, per_device(): summed = jnp.sum(lax.all_to_all(blocks, 'slab', 0, 0, tiled=True), axis=0)  6.78 us
  transfers between devices with their start and end apart: 5, of which 4 were waited for; matrix products, arithmetic and copies ran while one was open for 2% of the time, Pallas kernels for 14%

profile of v1, /device:TPU:0, one launch (start us, length us, event | category | flops | bytes accessed | tf_op | source)
XLA Modules:
  0.0 273.8 jit_solution(4726970080751181206)
XLA Ops:
  0.6 0.8 fusion.11
  1.4 0.7 convert_bitcast_fusion
  2.2 0.8 select_bitcast_fusion
  3.0 0.8 multiply_bitcast_fusion
  3.7 0.8 pad_maximum_fusion.1
  4.6 0.9 broadcast_in_dim.19
  5.5 7.3 %all-to-all-start = ((f32[8,96,256]{2,1,0:T(8,128)}), f32[8,96,256]{2,1,0:T(8,128)S(1)}, u32[]{:S(2)}, u32[]{:S(2)}) async-start(f32[8,96,256]{2,1,0:T(8,128)} %broadcast_in_dim.19), calls=%async_computation | async-start | bytes 1572864 | tf_op jit(solution)/shard_map/all_to_all | solution.py:545
  12.8 0.3 copy.105
  13.2 0.5 copy.106
  13.7 1.3 reshape.78
  14.9 18.0 %all-to-all-done = f32[8,96,256]{2,1,0:T(8,128)S(1)} async-done(((f32[8,96,256]{2,1,0:T(8,128)}), f32[8,96,256]{2,1,0:T(8,128)S(1)}, u32[]{:S(2)}, u32[]{:S(2)}) %all-to-all-start) | async-done | bytes 786464 | tf_op jit(solution)/shard_map/all_to_all | solution.py:545
  33.0 0.5 copy.104
  33.4 3.6 %all-to-all-start.1 = ((f32[8,64,256]{2,1,0:T(8,128)}), f32[8,64,256]{2,1,0:T(8,128)S(1)}, u32[]{:S(2)}, u32[]{:S(2)}) async-start(f32[8,64,256]{2,1,0:T(8,128)} %reshape.78), calls=%async_computation.1 | async-start | bytes 1048576 | tf_op jit(solution)/shard_map/all_to_all | solution.py:593
  37.0 0.3 copy.107.raw_ref
  37.3 0.3 convert_reduce_fusion
  37.6 0.3 slice_reduce_fusion
  38.1 7.8 %shard_map.158.geom_ref = f32[16,10,24,256]{3,2,1,0:T(8,128)S(1)} custom-call(s32[128]{0:T(128)S(1)} %concatenate.10.offsets, s32[16]{0:T(128)S(1)} %get-tuple-element.30.used, s32[1]{0:T(128)} %bitcast.7.own, f32[8,16,6,256]{3,2,1,0:T(8,128)S(1)} %copy.107.raw_ref), custom_call_target="tpu_custom_call" | custom-call | flops 4000000000 | bytes 10000000 | tf_op jit(solution)/shard_map/pallas_call | solution.py:531
  45.9 1.9 copy-done.14
  47.8 3.9 %all-to-all-done.1 = f32[8,64,256]{2,1,0:T(8,128)S(1)} async-done(((f32[8,64,256]{2,1,0:T(8,128)}), f32[8,64,256]{2,1,0:T(8,128)S(1)}, u32[]{:S(2)}, u32[]{:S(2)}) %all-to-all-start.1) | async-done | bytes 524320 | tf_op jit(solution)/shard_map/all_to_all | solution.py:593
  51.7 1.6 broadcast_in_dim.20
  53.3 3.8 %all-to-all-start.2 = ((f32[4,8,64,256]{3,2,1,0:T(8,128)}), f32[4,8,64,256]{3,2,1,0:T(8,128)S(1)}, u32[]{:S(2)}, u32[]{:S(2)}) async-start(f32[4,8,64,256]{3,2,1,0:T(8,128)} %broadcast_in_dim.20), calls=%async_computation.2 | async-start | bytes 4194304 | tf_op jit(solution)/shard_map/all_to_all | solution.py:557
  57.3 2.1 copy-done.15
  59.4 31.3 %shard_map.159.field_ref = f32[16,512,128]{2,1,0:T(8,128)S(1)} custom-call(s32[128]{0:T(128)S(1)} %concatenate.10.offsets, s32[16]{0:T(128)S(1)} %get-tuple-element.30.used, f32[16,10,24,256]{3,2,1,0:T(8,128)S(1)} %copy-done.15, f32[128,2,256]{2,1,0:T(2,128)S(1)} %bitcast.59), custom_call_target="tpu_custom_call" | custom-call | flops 4000000000 | bytes 10000000 | tf_op jit(solution)/shard_map/pallas_call | solution.py:531
  90.8 1.9 copy-done.12
  92.9 1.2 copy.142
  94.1 0.7 copy-done.13
  95.3 2.1 copy-done.16
  97.5 47.6 %shard_map.160 = f32[128,2,256]{2,1,0:T(2,128)} custom-call(s32[128]{0:T(128)S(1)} %concatenate.10.offsets, s32[16]{0:T(128)S(1)} %get-tuple-element.30.used, f32[16,10,24,256]{3,2,1,0:T(8,128)S(1)} %copy-done.16, f32[16,512,128]{2,1,0:T(8,128)S(1)} %copy-done.13, f32[16,128,256]{2,1,0:T(8,128)S(1)} %bitcast.56, bf16[256,768]{1,0:T(8,128)(2,1)S(1)} %copy-done.3, ...), custom_call_target="tpu_custom_call" | custom-call | flops 4000000000 | bytes 10000000 | tf_op jit(solution)/shard_map/pallas_call | solution.py:531
  145.1 4.0 %all-to-all-start.3 = ((f32[8,16,2,256]{3,2,1,0:T(2,128)}), f32[8,16,2,256]{3,2,1,0:T(2,128)}, u32[]{:S(2)}, u32[]{:S(2)}) async-start(f32[8,16,2,256]{3,2,1,0:T(2,128)} %bitcast.12), calls=%async_computation.3 | async-start | bytes 524288 | tf_op jit(solution)/shard_map/all_to_all | solution.py:647
  149.8 9.0 %all-to-all-done.3 = f32[8,16,2,256]{3,2,1,0:T(2,128)} async-done(((f32[8,16,2,256]{3,2,1,0:T(2,128)}), f32[8,16,2,256]{3,2,1,0:T(2,128)}, u32[]{:S(2)}, u32[]{:S(2)}) %all-to-all-start.3) | async-done | bytes 262176 | tf_op jit(solution)/shard_map/all_to_all | solution.py:647
  158.8 1.7 reduce_sum.76
  160.4 0.8 multiply_add_fusion
  161.4 12.5 %all_to_all.30 = f32[8,16,2,256]{3,2,1,0:T(2,128)S(1)} all-to-all(f32[8,16,2,256]{3,2,1,0:T(2,128)S(1)} %broadcast_in_dim.21), channel_id=1, replica_groups=mesh['slab'=8,'rhs'=4] {'slab'}, dimensions={0} | all-to-all | bytes 524288 | tf_op jit(solution)/shard_map/all_to_all | solution.py:545
  173.8 1.3 multiply_reduce_fusion.3
  175.2 1.2 multiply_reduce_fusion.2
  176.4 0.5 copy-done.29
  176.9 0.5 copy-done.27
  177.7 2.1 copy-done.17
  179.8 31.7 %shard_map.161.field_ref = f32[16,512,128]{2,1,0:T(8,128)S(1)} custom-call(s32[128]{0:T(128)S(1)} %concatenate.10.offsets, s32[16]{0:T(128)S(1)} %get-tuple-element.30.used, f32[16,10,24,256]{3,2,1,0:T(8,128)S(1)} %copy-done.17, f32[128,2,256]{2,1,0:T(2,128)S(1)} %fusion.1.vec_ref), custom_call_target="tpu_custom_call" | custom-call | flops 4000000000 | bytes 10000000 | tf_op jit(solution)/shard_map/pallas_call | solution.py:531
  211.5 46.9 %shard_map.162 = f32[128,2,256]{2,1,0:T(2,128)S(1)} custom-call(s32[128]{0:T(128)S(1)} %concatenate.10.offsets, s32[16]{0:T(128)S(1)} %get-tuple-element.30.used, f32[16,10,24,256]{3,2,1,0:T(8,128)S(1)} %copy-done.17, f32[16,512,128]{2,1,0:T(8,128)S(1)} %shard_map.161.field_ref, f32[16,128,256]{2,1,0:T(8,128)S(1)} %bitcast.57, ...), custom_call_target="tpu_custom_call" | custom-call | flops 4000000000 | bytes 10000000 | tf_op jit(solution)/shard_map/pallas_call | solution.py:531
  258.4 0.4 multiply_reduce_fusion.1
  258.9 0.8 pad_maximum_fusion
  259.7 3.6 %all-to-all-start.5 = ((f32[8,17,2,256]{3,2,1,0:T(2,128)}), f32[8,17,2,256]{3,2,1,0:T(2,128)S(1)}, u32[]{:S(2)}, u32[]{:S(2)}) async-start(f32[8,17,2,256]{3,2,1,0:T(2,128)} %pad_maximum_fusion), calls=%async_computation.5 | async-start | bytes 557056 | tf_op jit(solution)/shard_map/all_to_all | solution.py:663
  263.3 0.7 copy.116
  264.0 1.3 multiply_reduce_fusion
  265.4 6.8 %all-to-all-done.5 = f32[8,17,2,256]{3,2,1,0:T(2,128)S(1)} async-done(((f32[8,17,2,256]{3,2,1,0:T(2,128)}), f32[8,17,2,256]{3,2,1,0:T(2,128)S(1)}, u32[]{:S(2)}, u32[]{:S(2)}) %all-to-all-start.5) | async-done | bytes 278560 | tf_op jit(solution)/shard_map/all_to_all | solution.py:663
  272.4 0.7 fusion.10
  273.1 0.7 fusion.5
  (73 shorter events, 1.8 us)
Async XLA Ops:
  0.6 12.2 %copy-start.22 = (f32[2048,64]{0,1:T(8,128)S(1)}, f32[2048,64]{0,1:T(8,128)}, u32[]{:S(2)}) copy-start(f32[2048,64]{0,1:T(8,128)} %param.20) | copy-start | bytes 1572868
  1.4 4.1 %copy-start.20 = (f32[16,256]{1,0:T(8,128)}, f32[16,256]{1,0:T(8,128)S(1)}, u32[]{:S(2)}) copy-start(f32[16,256]{1,0:T(8,128)S(1)} %fusion.11) | copy-start | bytes 49156
  5.5 27.5 %all-to-all-start = ((f32[8,96,256]{2,1,0:T(8,128)}), f32[8,96,256]{2,1,0:T(8,128)S(1)}, u32[]{:S(2)}, u32[]{:S(2)}) async-start(f32[8,96,256]{2,1,0:T(8,128)} %broadcast_in_dim.19), calls=%async_computation | async-start | bytes 1572864 | tf_op jit(solution)/shard_map/all_to_all | solution.py:545
  33.4 23.7 %copy-start.18 = (f32[8,96,256]{2,0,1:T(8,128)}, f32[8,96,256]{2,0,1:T(8,128)S(1)}, u32[]{:S(2)}) copy-start(f32[8,96,256]{2,0,1:T(8,128)S(1)} %copy.104) | copy-start | bytes 2359300
  33.4 18.2 %all-to-all-start.1 = ((f32[8,64,256]{2,1,0:T(8,128)}), f32[8,64,256]{2,1,0:T(8,128)S(1)}, u32[]{:S(2)}, u32[]{:S(2)}) async-start(f32[8,64,256]{2,1,0:T(8,128)} %reshape.78), calls=%async_computation.1 | async-start | bytes 1048576 | tf_op jit(solution)/shard_map/all_to_all | solution.py:593
  45.9 1.9 copy-start.14
  53.3 39.4 %all-to-all-start.2 = ((f32[4,8,64,256]{3,2,1,0:T(8,128)}), f32[4,8,64,256]{3,2,1,0:T(8,128)S(1)}, u32[]{:S(2)}, u32[]{:S(2)}) async-start(f32[4,8,64,256]{3,2,1,0:T(8,128)} %broadcast_in_dim.20), calls=%async_computation.2 | async-start | bytes 4194304 | tf_op jit(solution)/shard_map/all_to_all | solution.py:557
  57.3 2.1 copy-start.15
  90.7 1.9 copy-start.12
  92.7 2.2 copy-start.13
  92.8 2.1 copy-start
  92.8 2.2 copy-start.1
  92.8 2.4 copy-start.2
  92.9 2.5 copy-start.3
  92.9 2.5 copy-start.5
  92.9 2.4 copy-start.7
  92.9 2.4 copy-start.9
  92.9 2.4 copy-start.10
  95.3 2.1 copy-start.16
  145.1 13.7 %all-to-all-start.3 = ((f32[8,16,2,256]{3,2,1,0:T(2,128)}), f32[8,16,2,256]{3,2,1,0:T(2,128)}, u32[]{:S(2)}, u32[]{:S(2)}) async-start(f32[8,16,2,256]{3,2,1,0:T(2,128)} %bitcast.12), calls=%async_computation.3 | async-start | bytes 524288 | tf_op jit(solution)/shard_map/all_to_all | solution.py:647
  173.8 3.1 %copy-start.19 = (f32[8,16,2,256]{3,2,1,0:T(2,128)}, f32[8,16,2,256]{3,2,1,0:T(2,128)S(1)}, u32[]{:S(2)}) copy-start(f32[8,16,2,256]{3,2,1,0:T(2,128)S(1)} %all_to_all.30) | copy-start | bytes 786436
  175.2 1.8 copy-start.25
  176.4 0.5 copy-start.29
  176.9 0.5 copy-start.27
  177.6 2.1 copy-start.17
  179.8 31.7 %copy-start.4 = (bf16[256,768]{1,0:T(8,128)(2,1)S(1)}, bf16[256,768]{1,0:T(8,128)(2,1)}, u32[]{:S(2)}) copy-start(bf16[256,768]{1,0:T(8,128)(2,1)} %constant.50.clone.row_fwd) | copy-start | bytes 1179652
  179.8 31.7 %copy-start.6 = (f32[128,128]{1,0:T(8,128)S(1)}, f32[128,128]{1,0:T(8,128)}, u32[]{:S(2)}) copy-start(f32[128,128]{1,0:T(8,128)} %constant.55.clone.mix_sin) | copy-start | bytes 196612
  179.8 31.7 %copy-start.8 = (f32[128,128]{1,0:T(8,128)S(1)}, f32[128,128]{1,0:T(8,128)}, u32[]{:S(2)}) copy-start(f32[128,128]{1,0:T(8,128)} %constant.54.clone.mix_cos) | copy-start | bytes 196612
  179.8 31.7 %copy-start.11 = (f32[16,128]{1,0:T(8,128)S(1)}, f32[16,128]{1,0:T(8,128)}, u32[]{:S(2)}) copy-start(f32[16,128]{1,0:T(8,128)} %constant.56.clone.turn_cos) | copy-start | bytes 24580
  258.3 14.0 %copy-start.21 = (f32[16,256]{1,0:T(8,128)S(1)}, f32[16,256]{1,0:T(8,128)}, u32[]{:S(2)}) copy-start(f32[16,256]{1,0:T(8,128)} %copy-done.20) | copy-start | bytes 49156
  258.3 14.1 %copy-start.23 = (f32[16,2,256]{2,1,0:T(2,128)S(1)}, f32[16,2,256]{2,1,0:T(2,128)}, u32[]{:S(2)}) copy-start(f32[16,2,256]{2,1,0:T(2,128)} %reduce_sum.76) | copy-start | bytes 98308
  258.4 14.1 %copy-start.24 = (f32[2,16,256]{2,1,0:T(8,128)S(1)}, f32[2,16,256]{2,1,0:T(8,128)}, u32[]{:S(2)}) copy-start(f32[2,16,256]{2,1,0:T(8,128)} %param.15) | copy-start | bytes 98308
  258.4 14.0 %copy-start.26 = (f32[2]{0:T(128)S(1)}, f32[2]{0:T(128)}, u32[]{:S(2)}) copy-start(f32[2]{0:T(128)} %copy-done.25) | copy-start | bytes 28
  258.4 14.0 %copy-start.28 = (f32[2]{0:T(128)S(1)}, f32[2]{0:T(128)}, u32[]{:S(2)}) copy-start(f32[2]{0:T(128)} %copy-done.27) | copy-start | bytes 28
  259.7 12.5 %all-to-all-start.5 = ((f32[8,17,2,256]{3,2,1,0:T(2,128)}), f32[8,17,2,256]{3,2,1,0:T(2,128)S(1)}, u32[]{:S(2)}, u32[]{:S(2)}) async-start(f32[8,17,2,256]{3,2,1,0:T(2,128)} %pad_maximum_fusion), calls=%async_computation.5 | async-start | bytes 557056 | tf_op jit(solution)/shard_map/all_to_all | solution.py:663

commit v2 on v1

--- a/solution.py
+++ b/solution.py
@@ -43,7 +43,7 @@
     out = []
     for sign in (1.0, -1.0):
         high, low = halves_np(np.block([[cos_t, sign * sin_t], [-sign * sin_t, cos_t]]))
-        out.append(np.concatenate([high, high, low], axis=1))
+        out.append(np.concatenate([high, low], axis=1))
     return out
 
 
@@ -52,7 +52,7 @@
     out = []
     for sign in (1.0, -1.0):
         high, low = halves_np(np.block([[cos_t, -sign * sin_t], [sign * sin_t, cos_t]]))
-        out.append(np.concatenate([high, high, low], axis=0))
+        out.append(np.concatenate([high, low], axis=0))
     return out
 
 
@@ -335,7 +335,8 @@
 
     def product_rows(matrix, columns):
         high, low = halves(jnp.concatenate(columns, axis=1))
-        result = dot_f32(matrix[...], jnp.concatenate([high, low, high], axis=0), ((1,), (0,)))
+        left = jnp.concatenate([matrix[:, :fold], matrix[...]], axis=1)
+        result = dot_f32(left, jnp.concatenate([high, low, high], axis=0), ((1,), (0,)))
         return [result[:, TC * i : TC * (i + 1)] for i in range(len(columns))]
 
     def rows_forward(group, carry):
@@ -411,7 +412,8 @@
     def lane_pass():
         def product(left, matrix):
             high, low = halves(left)
-            return dot_f32(jnp.concatenate([high, low, high], axis=1), matrix[...], ((1,), (0,)))
+            right = jnp.concatenate([matrix[:WIN], matrix[...]], axis=0)
+            return dot_f32(jnp.concatenate([high, low, high], axis=1), right, ((1,), (0,)))
 
         def step(group, carry):
             ats = [many * group + which for which in range(many)]

time: 274 us -> 275 us (level)
    unnamed x60 -> x54, local copies, waits for them, and re-layouts: 12.4 us -> 12.2 us
where the time goes in v2:
time: 275 us; the launch traced here: 273 us
  Pallas kernels  165 us (60%)
  waiting for transfers between devices  37.8 us (14%)
  starting transfers between devices  22.3 us (8%)
  local copies, waits for them, and re-layouts  20.5 us (7%)
  other arithmetic  13.6 us (5%)
  blocking collectives  12.5 us (5%)
    pallas_call x5, Pallas kernels, call_kernel(): pl.pallas_call(kernel, out_shape=jax.ShapeDtypeStruct(shape, jnp.float32)...  165 us
    all_to_all x1, waiting for transfers between devices, shared(): return lax.all_to_all(copies, 'slab', 0, 0, tiled=True)  18 us
    all_to_all x1, blocking collectives, shared(): return lax.all_to_all(copies, 'slab', 0, 0, tiled=True)  12.5 us
    unnamed x54, local copies, waits for them, and re-layouts  12.2 us
    all_to_all x1, waiting for transfers between devices, per_device(): smoothed = jnp.sum(lax.all_to_all(blocks, 'slab', 0, 0, tiled=True), axis=0)  9.01 us
    all_to_all x1, starting transfers between devices, shared(): return lax.all_to_all(copies, 'slab', 0, 0, tiled=True)  7.28 us
    all_to_all x1, waiting for transfers between devices, per_device(): summed = jnp.sum(lax.all_to_all(blocks, 'slab', 0, 0, tiled=True), axis=0)  6.76 us
  transfers between devices with their start and end apart: 5, of which 4 were waited for; matrix products, arithmetic and copies ran while one was open for 2% of the time, Pallas kernels for 14%

profile of v2, /device:TPU:0, one launch (start us, length us, event | category | flops | bytes accessed | tf_op | source)
XLA Modules:
  0.0 273.3 jit_solution(15674909690158982517)
XLA Ops:
  0.6 0.8 fusion.11
  1.4 0.7 convert_bitcast_fusion
  2.2 0.8 select_bitcast_fusion
  3.0 0.8 multiply_bitcast_fusion
  3.7 0.8 pad_maximum_fusion.1
  4.6 0.9 broadcast_in_dim.19
  5.5 7.3 %all-to-all-start = ((f32[8,96,256]{2,1,0:T(8,128)}), f32[8,96,256]{2,1,0:T(8,128)S(1)}, u32[]{:S(2)}, u32[]{:S(2)}) async-start(f32[8,96,256]{2,1,0:T(8,128)} %broadcast_in_dim.19), calls=%async_computation | async-start | bytes 1572864 | tf_op jit(solution)/shard_map/all_to_all | solution.py:547
  12.8 0.3 copy.105
  13.2 0.5 copy.106
  13.7 1.3 reshape.78
  14.9 18.0 %all-to-all-done = f32[8,96,256]{2,1,0:T(8,128)S(1)} async-done(((f32[8,96,256]{2,1,0:T(8,128)}), f32[8,96,256]{2,1,0:T(8,128)S(1)}, u32[]{:S(2)}, u32[]{:S(2)}) %all-to-all-start) | async-done | bytes 786464 | tf_op jit(solution)/shard_map/all_to_all | solution.py:547
  33.0 0.5 copy.104
  33.4 3.6 %all-to-all-start.1 = ((f32[8,64,256]{2,1,0:T(8,128)}), f32[8,64,256]{2,1,0:T(8,128)S(1)}, u32[]{:S(2)}, u32[]{:S(2)}) async-start(f32[8,64,256]{2,1,0:T(8,128)} %reshape.78), calls=%async_computation.1 | async-start | bytes 1048576 | tf_op jit(solution)/shard_map/all_to_all | solution.py:595
  37.0 0.3 copy.107.raw_ref
  37.3 0.3 convert_reduce_fusion
  37.6 0.3 slice_reduce_fusion
  38.1 7.8 %shard_map.158.geom_ref = f32[16,10,24,256]{3,2,1,0:T(8,128)S(1)} custom-call(s32[128]{0:T(128)S(1)} %concatenate.10.offsets, s32[16]{0:T(128)S(1)} %get-tuple-element.30.used, s32[1]{0:T(128)} %bitcast.7.own, f32[8,16,6,256]{3,2,1,0:T(8,128)S(1)} %copy.107.raw_ref), custom_call_target="tpu_custom_call" | custom-call | flops 4000000000 | bytes 10000000 | tf_op jit(solution)/shard_map/pallas_call | solution.py:533
  45.9 1.9 copy-done.11
  47.8 3.9 %all-to-all-done.1 = f32[8,64,256]{2,1,0:T(8,128)S(1)} async-done(((f32[8,64,256]{2,1,0:T(8,128)}), f32[8,64,256]{2,1,0:T(8,128)S(1)}, u32[]{:S(2)}, u32[]{:S(2)}) %all-to-all-start.1) | async-done | bytes 524320 | tf_op jit(solution)/shard_map/all_to_all | solution.py:595
  51.7 1.6 broadcast_in_dim.20
  53.3 3.8 %all-to-all-start.2 = ((f32[4,8,64,256]{3,2,1,0:T(8,128)}), f32[4,8,64,256]{3,2,1,0:T(8,128)S(1)}, u32[]{:S(2)}, u32[]{:S(2)}) async-start(f32[4,8,64,256]{3,2,1,0:T(8,128)} %broadcast_in_dim.20), calls=%async_computation.2 | async-start | bytes 4194304 | tf_op jit(solution)/shard_map/all_to_all | solution.py:559
  57.3 2.1 copy-done.12
  59.4 31.3 %shard_map.159.field_ref = f32[16,512,128]{2,1,0:T(8,128)S(1)} custom-call(s32[128]{0:T(128)S(1)} %concatenate.10.offsets, s32[16]{0:T(128)S(1)} %get-tuple-element.30.used, f32[16,10,24,256]{3,2,1,0:T(8,128)S(1)} %copy-done.12, f32[128,2,256]{2,1,0:T(2,128)S(1)} %bitcast.59), custom_call_target="tpu_custom_call" | custom-call | flops 4000000000 | bytes 10000000 | tf_op jit(solution)/shard_map/pallas_call | solution.py:533
  90.8 1.9 copy-done.9
  92.9 1.2 copy.142
  94.1 0.7 copy-done.10
  95.2 2.1 copy-done.13
  97.3 47.4 %shard_map.160 = f32[128,2,256]{2,1,0:T(2,128)} custom-call(s32[128]{0:T(128)S(1)} %concatenate.10.offsets, s32[16]{0:T(128)S(1)} %get-tuple-element.30.used, f32[16,10,24,256]{3,2,1,0:T(8,128)S(1)} %copy-done.13, f32[16,512,128]{2,1,0:T(8,128)S(1)} %copy-done.10, f32[16,128,256]{2,1,0:T(8,128)S(1)} %bitcast.56, bf16[256,512]{1,0:T(8,128)(2,1)S(1)} %copy-done.3, ...), custom_call_target="tpu_custom_call" | custom-call | flops 4000000000 | bytes 10000000 | tf_op jit(solution)/shard_map/pallas_call | solution.py:533
  144.7 4.0 %all-to-all-start.3 = ((f32[8,16,2,256]{3,2,1,0:T(2,128)}), f32[8,16,2,256]{3,2,1,0:T(2,128)}, u32[]{:S(2)}, u32[]{:S(2)}) async-start(f32[8,16,2,256]{3,2,1,0:T(2,128)} %bitcast.12), calls=%async_computation.3 | async-start | bytes 524288 | tf_op jit(solution)/shard_map/all_to_all | solution.py:649
  149.4 9.0 %all-to-all-done.3 = f32[8,16,2,256]{3,2,1,0:T(2,128)} async-done(((f32[8,16,2,256]{3,2,1,0:T(2,128)}), f32[8,16,2,256]{3,2,1,0:T(2,128)}, u32[]{:S(2)}, u32[]{:S(2)}) %all-to-all-start.3) | async-done | bytes 262176 | tf_op jit(solution)/shard_map/all_to_all | solution.py:649
  158.4 1.7 reduce_sum.76
  160.1 0.8 multiply_add_fusion
  161.0 12.5 %all_to_all.30 = f32[8,16,2,256]{3,2,1,0:T(2,128)S(1)} all-to-all(f32[8,16,2,256]{3,2,1,0:T(2,128)S(1)} %broadcast_in_dim.21), channel_id=1, replica_groups=mesh['slab'=8,'rhs'=4] {'slab'}, dimensions={0} | all-to-all | bytes 524288 | tf_op jit(solution)/shard_map/all_to_all | solution.py:547
  173.5 1.3 multiply_reduce_fusion.3
  174.8 1.2 multiply_reduce_fusion.2
  176.1 0.5 copy-done.26
  176.6 0.5 copy-done.24
  177.3 2.1 copy-done.14
  179.4 31.7 %shard_map.161.field_ref = f32[16,512,128]{2,1,0:T(8,128)S(1)} custom-call(s32[128]{0:T(128)S(1)} %concatenate.10.offsets, s32[16]{0:T(128)S(1)} %get-tuple-element.30.used, f32[16,10,24,256]{3,2,1,0:T(8,128)S(1)} %copy-done.14, f32[128,2,256]{2,1,0:T(2,128)S(1)} %fusion.1.vec_ref), custom_call_target="tpu_custom_call" | custom-call | flops 4000000000 | bytes 10000000 | tf_op jit(solution)/shard_map/pallas_call | solution.py:533
  211.1 46.8 %shard_map.162 = f32[128,2,256]{2,1,0:T(2,128)S(1)} custom-call(s32[128]{0:T(128)S(1)} %concatenate.10.offsets, s32[16]{0:T(128)S(1)} %get-tuple-element.30.used, f32[16,10,24,256]{3,2,1,0:T(8,128)S(1)} %copy-done.14, f32[16,512,128]{2,1,0:T(8,128)S(1)} %shard_map.161.field_ref, f32[16,128,256]{2,1,0:T(8,128)S(1)} %bitcast.57, ...), custom_call_target="tpu_custom_call" | custom-call | flops 4000000000 | bytes 10000000 | tf_op jit(solution)/shard_map/pallas_call | solution.py:533
  257.9 0.4 multiply_reduce_fusion.1
  258.4 0.8 pad_maximum_fusion
  259.2 3.6 %all-to-all-start.5 = ((f32[8,17,2,256]{3,2,1,0:T(2,128)}), f32[8,17,2,256]{3,2,1,0:T(2,128)S(1)}, u32[]{:S(2)}, u32[]{:S(2)}) async-start(f32[8,17,2,256]{3,2,1,0:T(2,128)} %pad_maximum_fusion), calls=%async_computation.5 | async-start | bytes 557056 | tf_op jit(solution)/shard_map/all_to_all | solution.py:665
  262.8 0.7 copy.116
  263.5 1.3 multiply_reduce_fusion
  264.9 6.8 %all-to-all-done.5 = f32[8,17,2,256]{3,2,1,0:T(2,128)S(1)} async-done(((f32[8,17,2,256]{3,2,1,0:T(2,128)}), f32[8,17,2,256]{3,2,1,0:T(2,128)S(1)}, u32[]{:S(2)}, u32[]{:S(2)}) %all-to-all-start.5) | async-done | bytes 278560 | tf_op jit(solution)/shard_map/all_to_all | solution.py:665
  271.9 0.7 fusion.10
  272.6 0.7 fusion.5
  (67 shorter events, 1.6 us)
Async XLA Ops:
  0.6 12.2 %copy-start.19 = (f32[2048,64]{0,1:T(8,128)S(1)}, f32[2048,64]{0,1:T(8,128)}, u32[]{:S(2)}) copy-start(f32[2048,64]{0,1:T(8,128)} %param.20) | copy-start | bytes 1572868
  1.4 4.1 %copy-start.17 = (f32[16,256]{1,0:T(8,128)}, f32[16,256]{1,0:T(8,128)S(1)}, u32[]{:S(2)}) copy-start(f32[16,256]{1,0:T(8,128)S(1)} %fusion.11) | copy-start | bytes 49156
  5.5 27.5 %all-to-all-start = ((f32[8,96,256]{2,1,0:T(8,128)}), f32[8,96,256]{2,1,0:T(8,128)S(1)}, u32[]{:S(2)}, u32[]{:S(2)}) async-start(f32[8,96,256]{2,1,0:T(8,128)} %broadcast_in_dim.19), calls=%async_computation | async-start | bytes 1572864 | tf_op jit(solution)/shard_map/all_to_all | solution.py:547
  33.4 23.7 %copy-start.15 = (f32[8,96,256]{2,0,1:T(8,128)}, f32[8,96,256]{2,0,1:T(8,128)S(1)}, u32[]{:S(2)}) copy-start(f32[8,96,256]{2,0,1:T(8,128)S(1)} %copy.104) | copy-start | bytes 2359300
  33.4 18.2 %all-to-all-start.1 = ((f32[8,64,256]{2,1,0:T(8,128)}), f32[8,64,256]{2,1,0:T(8,128)S(1)}, u32[]{:S(2)}, u32[]{:S(2)}) async-start(f32[8,64,256]{2,1,0:T(8,128)} %reshape.78), calls=%async_computation.1 | async-start | bytes 1048576 | tf_op jit(solution)/shard_map/all_to_all | solution.py:595
  45.9 1.9 copy-start.11
  53.3 39.4 %all-to-all-start.2 = ((f32[4,8,64,256]{3,2,1,0:T(8,128)}), f32[4,8,64,256]{3,2,1,0:T(8,128)S(1)}, u32[]{:S(2)}, u32[]{:S(2)}) async-start(f32[4,8,64,256]{3,2,1,0:T(8,128)} %broadcast_in_dim.20), calls=%async_computation.2 | async-start | bytes 4194304 | tf_op jit(solution)/shard_map/all_to_all | solution.py:559
  57.3 2.1 copy-start.12
  90.7 1.9 copy-start.9
  92.7 2.2 copy-start.10
  92.8 2.1 copy-start
  92.8 2.2 copy-start.1
  92.8 2.2 copy-start.2
  92.9 2.3 copy-start.3
  92.9 2.3 copy-start.4
  92.9 2.3 copy-start.5
  92.9 2.3 copy-start.6
  92.9 2.3 copy-start.7
  95.2 2.1 copy-start.13
  144.7 13.7 %all-to-all-start.3 = ((f32[8,16,2,256]{3,2,1,0:T(2,128)}), f32[8,16,2,256]{3,2,1,0:T(2,128)}, u32[]{:S(2)}, u32[]{:S(2)}) async-start(f32[8,16,2,256]{3,2,1,0:T(2,128)} %bitcast.12), calls=%async_computation.3 | async-start | bytes 524288 | tf_op jit(solution)/shard_map/all_to_all | solution.py:649
  173.5 3.1 %copy-start.16 = (f32[8,16,2,256]{3,2,1,0:T(2,128)}, f32[8,16,2,256]{3,2,1,0:T(2,128)S(1)}, u32[]{:S(2)}) copy-start(f32[8,16,2,256]{3,2,1,0:T(2,128)S(1)} %all_to_all.30) | copy-start | bytes 786436
  174.8 1.8 copy-start.22
  176.1 0.5 copy-start.26
  176.6 0.5 copy-start.24
  177.3 2.1 copy-start.14
  179.4 31.7 %copy-start.8 = (f32[16,128]{1,0:T(8,128)S(1)}, f32[16,128]{1,0:T(8,128)}, u32[]{:S(2)}) copy-start(f32[16,128]{1,0:T(8,128)} %constant.56.clone.turn_cos) | copy-start | bytes 24580
  257.9 14.0 %copy-start.18 = (f32[16,256]{1,0:T(8,128)S(1)}, f32[16,256]{1,0:T(8,128)}, u32[]{:S(2)}) copy-start(f32[16,256]{1,0:T(8,128)} %copy-done.17) | copy-start | bytes 49156
  257.9 14.0 %copy-start.20 = (f32[16,2,256]{2,1,0:T(2,128)S(1)}, f32[16,2,256]{2,1,0:T(2,128)}, u32[]{:S(2)}) copy-start(f32[16,2,256]{2,1,0:T(2,128)} %reduce_sum.76) | copy-start | bytes 98308
  257.9 14.0 %copy-start.21 = (f32[2,16,256]{2,1,0:T(8,128)S(1)}, f32[2,16,256]{2,1,0:T(8,128)}, u32[]{:S(2)}) copy-start(f32[2,16,256]{2,1,0:T(8,128)} %param.15) | copy-start | bytes 98308
  257.9 14.0 %copy-start.23 = (f32[2]{0:T(128)S(1)}, f32[2]{0:T(128)}, u32[]{:S(2)}) copy-start(f32[2]{0:T(128)} %copy-done.22) | copy-start | bytes 28
  257.9 14.0 %copy-start.25 = (f32[2]{0:T(128)S(1)}, f32[2]{0:T(128)}, u32[]{:S(2)}) copy-start(f32[2]{0:T(128)} %copy-done.24) | copy-start | bytes 28
  259.2 12.5 %all-to-all-start.5 = ((f32[8,17,2,256]{3,2,1,0:T(2,128)}), f32[8,17,2,256]{3,2,1,0:T(2,128)S(1)}, u32[]{:S(2)}, u32[]{:S(2)}) async-start(f32[8,17,2,256]{3,2,1,0:T(2,128)} %pad_maximum_fusion), calls=%async_computation.5 | async-start | bytes 557056 | tf_op jit(solution)/shard_map/all_to_all | solution.py:665
